TPU v7x, 256 devices: a whole 4x4x8 slice. The times are simulated.
256 devices in a mesh: island: 8 (over z_hi, x), row: 8 (over y, core), col: 4 (over z_lo).
Axes of the slice: x: 4, y: 4, z: 8 (z_hi: 2, z_lo: 4; z = z_hi * 4 + z_lo), core: 2. Of those that a mesh axis runs over, the one named last changes fastest.
Arguments:
- deltas: float32 [8, 4096, 8192], P('island', 'row', 'col'), may hold values from -0.26516503 to 0.26516503
- left_stat: float32 [4096, 4096], P(('island', 'col'), 'row'), may hold values from -1.5 to 1.5
- right_stat: float32 [8192, 8192], P(('island', 'row'), 'col'), may hold values from -1.5 to 1.5
Outputs:
- left_new: float32 [4096, 4096], P(('island', 'col'), 'row')
- right_new: float32 [8192, 8192], P(('island', 'row'), 'col')
All inputs are finite; a program needn't handle non-finite values.
Results may differ from a plain program's by a relative error of at most 0.00037.
Values may be sent and summed in bfloat16 or wider, within the bound.
No kernel may reach another device: no remote copies, remote signals or barrier semaphores. Data moves between devices by JAX's collectives and lax.ppermute only.
A program may use at most 64 MiB of HBM per device.

v0:
```python
import jax
import jax.numpy as jnp
from jax import lax
from jax.sharding import PartitionSpec as P

M = 4096
N = 8192


def padded_to(lines, count):
    spare = -lines.shape[0] % count
    if not spare:
        return lines
    return jnp.concatenate([lines, jnp.zeros((spare, *lines.shape[1:]), lines.dtype)])


def broadcast_by_parts(shard, axis, root):
    lines = jnp.where(lax.axis_index(axis) == root, shard, jnp.zeros_like(shard)).reshape(
        -1, *shard.shape[1:][-1:]
    )
    padded = padded_to(lines, lax.axis_size(axis))
    own = lax.psum_scatter(padded, axis, scatter_dimension=0, tiled=True)
    return lax.all_gather(own, axis, axis=0, tiled=True)[: len(lines)].reshape(shard.shape)


def split_up(shard, dim, count):
    before, after = (shard.shape[:dim], shard.shape[dim + 1 :])
    return jnp.moveaxis(shard.reshape(*before, count, -1, *after), dim, 0)


def summed_on_arrival(shard, axis, dim):
    tiles = split_up(shard, dim, lax.axis_size(axis))
    arrived = lax.all_to_all(tiles, axis, split_axis=0, concat_axis=0, tiled=True)
    return arrived.sum(axis=0)


def from_root(shard, axis, root):
    return lax.dynamic_index_in_dim(lax.all_gather(shard, axis), root, 0, keepdims=False)


def local(deltas, left_stat, right_stat):
    islands = lax.axis_size("island")
    island = lax.axis_index("island")
    local_delta = deltas[0]
    shares = lax.psum_scatter(local_delta, "island", scatter_dimension=0, tiled=True)
    rounded = (shares / islands).astype(jnp.bfloat16)
    panel = lax.all_gather(rounded, "island", axis=0, tiled=True)
    rows_local = panel.shape[0]
    rows_island = M // islands
    row_extent = min(rows_island, rows_local)
    number = 0
    start_row = island * rows_island + number * row_extent
    source = start_row // rows_local
    segment = panel
    blocks = broadcast_by_parts(segment, "row", source)
    left_tile = lax.dot_general(
        blocks, panel, (((1,), (1,)), ((), ())), preferred_element_type=jnp.float32
    )
    left_shares = summed_on_arrival(left_tile, "col", 0)
    left_new = left_stat + left_shares
    cols_local = panel.shape[1]
    cols_island = N // islands
    col_extent = min(cols_island, cols_local)
    number = 0
    start_col = island * cols_island + number * col_extent
    source = start_col // cols_local
    offset = start_col - source * cols_local
    segment = lax.dynamic_slice_in_dim(panel, offset, col_extent, 1)
    columns = from_root(segment, "col", source)
    right_tile = lax.dot_general(
        columns, panel, (((0,), (0,)), ((), ())), preferred_element_type=jnp.float32
    )
    right_shares = lax.psum_scatter(right_tile, "row", scatter_dimension=0, tiled=True)
    right_new = right_stat + right_shares
    return (left_new, right_new)


def solution(mesh):
    in_specs = (P("island", "row", "col"), P(("island", "col"), "row"), P(("island", "row"), "col"))
    out_specs = (P(("island", "col"), "row"), P(("island", "row"), "col"))
    return jax.shard_map(local, mesh=mesh, in_specs=in_specs, out_specs=out_specs, check_vma=False)
```

profile of v0, /device:TPU:1, one launch (start us, length us, event | category | flops | bytes accessed | tf_op | source)
XLA Modules:
  0.0 430.5 jit_solution(14289214902869584653)
XLA Ops:
  7.2 0.0 reduce-scatter.4.cloned.1.call-start
  7.2 0.7 reduce-scatter.4.cloned.1.call-update
  7.9 0.0 all-gather.5.cloned.1.call-start
  7.9 129.9 %reduce-scatter.4.cloned.1.call-done = f32[64,2048]{1,0:T(8,128)} async-done(((f32[512,2048]{1,0:T(8,128)}), f32[64,2048]{1,0:T(8,128)}) %reduce-scatter.4.cloned.1.call-update) | async-done | bytes 524304 | tf_op jit(solution)/shard_map/reduce_scatter | solution.py:45
  137.9 1.8 multiply_convert_fusion
  139.6 0.0 all-gather.5.cloned.1.call-update
  139.7 0.0 reduce-scatter.6.cloned.1.call-start
  139.7 72.0 %all-gather.5.cloned.1.call-done = bf16[512,2048]{1,0:T(8,128)(2,1)} async-done(((bf16[64,2048]{1,0:T(8,128)(2,1)}), bf16[512,2048]{1,0:T(8,128)(2,1)}) %all-gather.5.cloned.1.call-update) | async-done | bytes 2097168 | tf_op jit(solution)/shard_map/all_gather | solution.py:47
  211.7 1.5 broadcast_select_fusion
  213.2 0.0 copy-start
  213.2 0.0 reduce-scatter.6.cloned.1.call-update
  213.2 0.0 all-gather.9.cloned.1.call-start
  213.3 1.5 copy-done
  214.8 1.1 constant_dynamic-slice_fusion
  215.9 0.0 all-gather.9.cloned.1.call-update
  215.9 0.0 all-gather.7.cloned.1.call-start
  215.9 30.9 %reduce-scatter.6.cloned.1.call-done = bf16[64,2048]{1,0:T(8,128)(2,1)} async-done(((bf16[512,2048]{1,0:T(8,128)(2,1)}), bf16[64,2048]{1,0:T(8,128)(2,1)}) %reduce-scatter.6.cloned.1.call-update) | async-done | bytes 262160 | tf_op jit(solution)/shard_map/reduce_scatter | solution.py:22
  246.8 0.0 all-gather.7.cloned.1.call-update
  246.8 0.0 reduce-scatter.8.cloned.1.call-start
  246.9 87.2 %all-gather.9.cloned.1.call-done = bf16[2048,1024]{1,0:T(8,128)(2,1)} async-done(((bf16[512,1024]{1,0:T(8,128)(2,1)}), bf16[2048,1024]{1,0:T(8,128)(2,1)}) %all-gather.9.cloned.1.call-update) | async-done | bytes 4194320 | tf_op jit(solution)/shard_map/all_gather | solution.py:38
  334.1 6.8 %fusion = f32[1024,2048]{1,0:T(8,128)} fusion(bf16[512,2048]{1,0:T(8,128)(2,1)S(1)} %copy-done, bf16[4,512,1024]{2,1,0:T(8,128)(2,1)} %bitcast.11, s32[]{:T(128)S(6)} %select_n.28), kind=kOutput, calls=%fused_computation.1 | convolution fusion | flops 2147483648 | bytes 11534340 | tf_op jit(solution)/shard_map/dot_general | solution.py:70
  340.9 0.0 reduce-scatter.8.cloned.1.call-update
  340.9 23.5 %all-gather.7.cloned.1.call-done = bf16[512,2048]{1,0:T(8,128)(2,1)} async-done(((bf16[64,2048]{1,0:T(8,128)(2,1)}), bf16[512,2048]{1,0:T(8,128)(2,1)}) %all-gather.7.cloned.1.call-update) | async-done | bytes 2097168 | tf_op jit(solution)/shard_map/all_gather | solution.py:23
  364.4 2.9 fusion.4
  367.3 0.0 copy-start.2
  367.3 0.0 copy-start.1
  367.3 29.8 %all_to_all.5 = f32[4,128,512]{2,1,0:T(8,128)S(1)} all-to-all(f32[4,128,512]{2,1,0:T(8,128)S(1)} %bitcast.10), channel_id=1, replica_groups=mesh['island'=8,'row'=8,'col'=4] {'col'}, dimensions={0} | all-to-all | bytes 2097152 | tf_op jit(solution)/shard_map/all_to_all | solution.py:33
  397.2 0.1 reduce_sum.9
  397.3 0.0 copy-done.2
  397.3 0.7 add.21
  398.0 23.3 %reduce-scatter.8.cloned.1.call-done = f32[128,2048]{1,0:T(8,128)} async-done(((f32[1024,2048]{1,0:T(8,128)}), f32[128,2048]{1,0:T(8,128)}) %reduce-scatter.8.cloned.1.call-update) | async-done | bytes 1048592 | tf_op jit(solution)/shard_map/reduce_scatter | solution.py:73
  421.3 0.0 copy-done.1
  421.3 2.3 add.24
Async XLA Ops:
  7.2 130.7 %reduce-scatter.4.cloned.1.call-start = ((), (), s32[]{:S(2)}) async-start(), calls=%async_computation.4 | async-start | bytes 4718592 | tf_op jit(solution)/shard_map/reduce_scatter | solution.py:45
  7.9 203.8 %all-gather.5.cloned.1.call-start = ((), (), s32[]{:S(2)}) async-start(), calls=%async_computation.5 | async-start | bytes 2359296 | tf_op jit(solution)/shard_map/all_gather | solution.py:47
  139.7 107.1 %reduce-scatter.6.cloned.1.call-start = ((), (), s32[]{:S(2)}) async-start(), calls=%async_computation.6 | async-start | bytes 2359296 | tf_op jit(solution)/shard_map/reduce_scatter | solution.py:22
  213.2 1.6 copy-start
  213.2 120.9 %all-gather.9.cloned.1.call-start = ((), (), s32[]{:S(2)}) async-start(), calls=%async_computation.9 | async-start | bytes 5242880 | tf_op jit(solution)/shard_map/all_gather | solution.py:38
  215.9 148.5 %all-gather.7.cloned.1.call-start = ((), (), s32[]{:S(2)}) async-start(), calls=%async_computation.7 | async-start | bytes 2359296 | tf_op jit(solution)/shard_map/all_gather | solution.py:23
  246.8 174.5 %reduce-scatter.8.cloned.1.call-start = ((), (), s32[]{:S(2)}) async-start(), calls=%async_computation.8 | async-start | bytes 9437184 | tf_op jit(solution)/shard_map/reduce_scatter | solution.py:73
  367.3 30.0 %copy-start.2 = (f32[128,512]{1,0:T(8,128)S(1)}, f32[128,512]{1,0:T(8,128)}, u32[]{:S(2)}) copy-start(f32[128,512]{1,0:T(8,128)} %param.4) | copy-start | bytes 786436
  367.3 54.0 %copy-start.1 = (f32[128,2048]{1,0:T(8,128)S(1)}, f32[128,2048]{1,0:T(8,128)}, u32[]{:S(2)}) copy-start(f32[128,2048]{1,0:T(8,128)} %param.5) | copy-start | bytes 3145732
Sparse Core Ops, SparseCore 0:
  12.1 125.6 reduce-scatter.3
  141.1 70.6 all-gather.4
  214.3 32.4 reduce-scatter.5
  249.0 84.9 all-gather.8
  335.8 28.5 all-gather.6
  366.8 54.4 reduce-scatter.7
where the time goes:
time: 431 us; the launch traced here: 430 us
  waiting for transfers between devices  368 us (85%)
  blocking collectives  29.8 us (7%)
  between operations  14.2 us (3%)
  matrix products  9.71 us (2%)
  other arithmetic  6.39 us (1%)
    reduce_scatter x1, waiting for transfers between devices, local(): lax.psum_scatter(local_delta, 'island', scatter_dimension=0, tiled=True)  130 us
    all_gather x1, waiting for transfers between devices, from_root(): lax.all_gather(shard, axis)  87.2 us
    all_gather x1, waiting for transfers between devices, local(): panel = lax.all_gather(rounded, 'island', axis=0, tiled=True)  72 us
    reduce_scatter x1, waiting for transfers between devices, broadcast_by_parts(): own = lax.psum_scatter(padded, axis, scatter_dimension=0, tiled=True)  30.9 us
    all_to_all x1, blocking collectives, summed_on_arrival(): lax.all_to_all(tiles, axis, split_axis=0, concat_axis=0, tiled=True)  29.8 us
    all_gather x1, waiting for transfers between devices, broadcast_by_parts(): lax.all_gather(own, axis, axis=0, tiled=True)[:len(lines)]  23.5 us
    reduce_scatter x1, waiting for transfers between devices, local(): lax.psum_scatter(right_tile, 'row', scatter_dimension=0, tiled=True)  23.3 us
  transfers between devices with their start and end apart: 6, of which 6 were waited for; matrix products, arithmetic and copies ran while one was open for 3% of the time, Pallas kernels for 0%

commit v1 on v0

--- a/solution.py
+++ b/solution.py
@@ -20,7 +20,19 @@
     )
     padded = padded_to(lines, lax.axis_size(axis))
     own = lax.psum_scatter(padded, axis, scatter_dimension=0, tiled=True)
-    return lax.all_gather(own, axis, axis=0, tiled=True)[: len(lines)].reshape(shard.shape)
+
+    def name_ticks_all(block_in, shard_axis):
+        return jnp.concatenate(
+            jax.lax.all_to_all(
+                jnp.stack(jax.lax.axis_size(shard_axis) * [block_in], axis=0),
+                shard_axis,
+                concat_axis=0,
+                split_axis=0,
+            ),
+            0,
+        )
+
+    return name_ticks_all(own, axis)[: len(lines)].reshape(shard.shape)
 
 
 def split_up(shard, dim, count):

time: 431 us -> 415 us (0.963)
  waiting for transfers between devices: 368 us -> 314 us
  blocking collectives: 29.8 us -> 68.9 us
    all_to_all x0 -> x1, blocking collectives: none -> 39.2 us  [name_ticks_all(): jax.lax.all_to_all(jnp.stack(jax.lax.axis_size(shard_axis) * [block_in],...]
    all_gather x1 -> x0, waiting for transfers between devices: 23.5 us -> none  [broadcast_by_parts(): lax.all_gather(own, axis, axis=0, tiled=True)[:len(lines)]]
    reduce_scatter x1, waiting for transfers between devices: 23.3 us -> 0.56 us  [local(): lax.psum_scatter(right_tile, 'row', scatter_dimension=0, tiled=True)]
    all_gather x1, waiting for transfers between devices: 87.2 us -> 80.8 us  [from_root(): lax.all_gather(shard, axis)]
  transfers between devices with their start and end apart: 6 -> 5, of which waited for: 6 -> 5; matrix products, arithmetic and copies ran while one was open for 3% -> 3% of each run, Pallas kernels for 0% -> 0%
where the time goes in v1:
time: 415 us
  waiting for transfers between devices  314 us (76%)
  blocking collectives  68.9 us (17%)
  between operations  13.9 us (3%)
  matrix products  8.12 us (2%)
  other arithmetic  6.38 us (2%)
    reduce_scatter x1, waiting for transfers between devices, local(): lax.psum_scatter(local_delta, 'island', scatter_dimension=0, tiled=True)  130 us
    all_gather x1, waiting for transfers between devices, from_root(): lax.all_gather(shard, axis)  80.8 us
    all_gather x1, waiting for transfers between devices, local(): panel = lax.all_gather(rounded, 'island', axis=0, tiled=True)  72 us
    all_to_all x1, blocking collectives, name_ticks_all(): jax.lax.all_to_all(jnp.stack(jax.lax.axis_size(shard_axis) * [block_in],...  39.2 us
    reduce_scatter x1, waiting for transfers between devices, broadcast_by_parts(): own = lax.psum_scatter(padded, axis, scatter_dimension=0, tiled=True)  29.9 us
    all_to_all x1, blocking collectives, summed_on_arrival(): lax.all_to_all(tiles, axis, split_axis=0, concat_axis=0, tiled=True)  29.7 us
  transfers between devices with their start and end apart: 5, of which 5 were waited for; matrix products, arithmetic and copies ran while one was open for 3% of the time, Pallas kernels for 0%

profile of v1, /device:TPU:1, one launch (start us, length us, event | category | flops | bytes accessed | tf_op | source)
XLA Modules:
  0.0 414.9 jit_solution(16547493332652149022)
XLA Ops:
  7.2 0.0 reduce-scatter.4.cloned.1.call-start
  7.2 0.7 reduce-scatter.4.cloned.1.call-update
  7.9 0.0 all-gather.4.cloned.1.call-start
  7.9 129.9 %reduce-scatter.4.cloned.1.call-done = f32[64,2048]{1,0:T(8,128)} async-done(((f32[512,2048]{1,0:T(8,128)}), f32[64,2048]{1,0:T(8,128)}) %reduce-scatter.4.cloned.1.call-update) | async-done | bytes 524304 | tf_op jit(solution)/shard_map/reduce_scatter | solution.py:57
  137.9 1.8 multiply_convert_fusion
  139.6 0.0 all-gather.4.cloned.1.call-update
  139.7 0.0 all-gather.6.cloned.1.call-start
  139.7 72.0 %all-gather.4.cloned.1.call-done = bf16[512,2048]{1,0:T(8,128)(2,1)} async-done(((bf16[64,2048]{1,0:T(8,128)(2,1)}), bf16[512,2048]{1,0:T(8,128)(2,1)}) %all-gather.4.cloned.1.call-update) | async-done | bytes 2097168 | tf_op jit(solution)/shard_map/all_gather | solution.py:59
  211.7 0.0 copy-start
  211.7 2.4 constant_dynamic-slice_fusion
  214.1 0.0 all-gather.6.cloned.1.call-update
  214.2 0.0 reduce-scatter.6.cloned.1.call-start
  214.2 0.0 copy-done
  214.2 1.5 broadcast_select_fusion
  215.7 0.0 reduce-scatter.6.cloned.1.call-update
  215.7 0.0 reduce-scatter.8.cloned.1.call-start
  215.8 80.8 %all-gather.6.cloned.1.call-done = bf16[2048,1024]{1,0:T(8,128)(2,1)} async-done(((bf16[512,1024]{1,0:T(8,128)(2,1)}), bf16[2048,1024]{1,0:T(8,128)(2,1)}) %all-gather.6.cloned.1.call-update) | async-done | bytes 4194320 | tf_op jit(solution)/shard_map/all_gather | solution.py:50
  296.6 6.8 %fusion.2 = f32[1024,2048]{1,0:T(8,128)} fusion(bf16[512,2048]{1,0:T(8,128)(2,1)S(1)} %copy-done, bf16[4,512,1024]{2,1,0:T(8,128)(2,1)} %bitcast.13, s32[]{:T(128)S(6)} %select_n.28), kind=kOutput, calls=%fused_computation.3 | convolution fusion | flops 2147483648 | bytes 11534340 | tf_op jit(solution)/shard_map/dot_general | solution.py:82
  303.4 0.0 reduce-scatter.8.cloned.1.call-update
  303.4 29.9 %reduce-scatter.6.cloned.1.call-done = bf16[64,2048]{1,0:T(8,128)(2,1)} async-done(((bf16[512,2048]{1,0:T(8,128)(2,1)}), bf16[64,2048]{1,0:T(8,128)(2,1)}) %reduce-scatter.6.cloned.1.call-update) | async-done | bytes 262160 | tf_op jit(solution)/shard_map/reduce_scatter | solution.py:22
  333.3 1.2 stack.2
  334.5 39.2 %all_to_all.10 = bf16[8,64,2048]{2,1,0:T(8,128)(2,1)S(1)} all-to-all(bf16[8,64,2048]{2,1,0:T(8,128)(2,1)S(1)} %stack.2), channel_id=1, replica_groups=mesh['island'=8,'row'=8,'col'=4] {'row'}, dimensions={0} | all-to-all | bytes 4194304 | tf_op jit(solution)/shard_map/all_to_all | solution.py:26
  373.7 1.3 fusion
  375.0 0.0 copy-start.2
  375.0 0.0 copy-start.1
  375.0 29.7 %all_to_all.11 = f32[4,128,512]{2,1,0:T(8,128)S(1)} all-to-all(f32[4,128,512]{2,1,0:T(8,128)S(1)} %fusion), channel_id=1, replica_groups=mesh['island'=8,'row'=8,'col'=4] {'col'}, dimensions={0} | all-to-all | bytes 2097152 | tf_op jit(solution)/shard_map/all_to_all | solution.py:45
  404.7 0.1 reduce_sum.9
  404.8 0.0 copy-done.2
  404.8 0.7 add.21
  405.5 0.6 reduce-scatter.8.cloned.1.call-done
  406.1 0.0 copy-done.1
  406.1 2.3 add.24
Async XLA Ops:
  7.2 130.7 %reduce-scatter.4.cloned.1.call-start = ((), (), s32[]{:S(2)}) async-start(), calls=%async_computation.5 | async-start | bytes 4718592 | tf_op jit(solution)/shard_map/reduce_scatter | solution.py:57
  7.9 203.8 %all-gather.4.cloned.1.call-start = ((), (), s32[]{:S(2)}) async-start(), calls=%async_computation.6 | async-start | bytes 2359296 | tf_op jit(solution)/shard_map/all_gather | solution.py:59
  139.7 156.9 %all-gather.6.cloned.1.call-start = ((), (), s32[]{:S(2)}) async-start(), calls=%async_computation.9 | async-start | bytes 5242880 | tf_op jit(solution)/shard_map/all_gather | solution.py:50
  211.7 2.5 copy-start
  214.2 119.1 %reduce-scatter.6.cloned.1.call-start = ((), (), s32[]{:S(2)}) async-start(), calls=%async_computation.7 | async-start | bytes 2359296 | tf_op jit(solution)/shard_map/reduce_scatter | solution.py:22
  215.7 190.4 %reduce-scatter.8.cloned.1.call-start = ((), (), s32[]{:S(2)}) async-start(), calls=%async_computation.8 | async-start | bytes 9437184 | tf_op jit(solution)/shard_map/reduce_scatter | solution.py:85
  375.0 29.8 %copy-start.2 = (f32[128,512]{1,0:T(8,128)S(1)}, f32[128,512]{1,0:T(8,128)}, u32[]{:S(2)}) copy-start(f32[128,512]{1,0:T(8,128)} %param.4) | copy-start | bytes 786436
  375.0 31.1 %copy-start.1 = (f32[128,2048]{1,0:T(8,128)S(1)}, f32[128,2048]{1,0:T(8,128)}, u32[]{:S(2)}) copy-start(f32[128,2048]{1,0:T(8,128)} %param.5) | copy-start | bytes 3145732
Sparse Core Ops, SparseCore 0:
  12.1 125.6 reduce-scatter.3
  141.1 70.6 all-gather.3
  214.3 82.2 all-gather.5
  299.0 34.2 reduce-scatter.5
  335.7 70.3 reduce-scatter.7
